TPU v7x, 256 devices: a whole 4x4x8 slice. The times are simulated.
256 devices in a mesh: mb: 8 (over z), tp: 8 (over y, core), dp: 4 (over x).
Axes of the slice: x: 4, y: 4, z: 8, core: 2. Of those that a mesh axis runs over, the one named last changes fastest.
Arguments:
- hidden: bfloat16 [4, 16, 512, 7168], P('dp', 'mb', None, 'tp'), may hold values from -6 to 6
- latent: bfloat16 [4, 16, 512, 512], P('dp', 'mb', None, 'tp'), may hold values from -6 to 6
- out_grad: bfloat16 [4, 16, 512, 16384], P('dp', 'mb', None, 'tp'), may hold values from -0.059814453 to 0.059814453
- up_weight: bfloat16 [512, 16384], P(None, 'tp'), may hold values from -0.046875 to 0.046875
- mb_tokens: int32 [4, 16], P('dp'), may hold values from 128 to 512, as said below
- slot_mb: int32 [4, 16], P('dp', 'mb'), may hold values from 0 to 15, each once within a row
Outputs:
- up_grad: float32 [512, 16384], P(('mb', 'dp'), 'tp')
- running_down: float32 [8, 7168, 512], P('mb', 'tp', 'dp')
Inputs may be any that keep to these rules, and one draw needn't show every extreme that they name: `mb_tokens`: each count is a multiple of 128; in every group some microbatch has exactly 512 tokens. `slot_mb`: each row is a permutation of the microbatch numbers.
All inputs are finite; a program needn't handle non-finite values.
Results may differ from a plain program's by a relative error of at most 0.005.
Values may be sent and summed in bfloat16 or wider, within the bound.
A program may use at most 128 MiB of HBM per device.

v0:
```python
import jax
import jax.numpy as jnp
from jax import lax
from jax.sharding import PartitionSpec as P


def copy_for_each(value, axis):
    copies = jnp.broadcast_to(value, (lax.axis_size(axis), *value.shape))
    return lax.all_to_all(copies, axis, split_axis=0, concat_axis=0, tiled=True)


def laid_out(blocks, dim):
    blocks = jnp.moveaxis(blocks, 0, dim)
    dims = blocks.shape
    return blocks.reshape(*dims[:dim], dims[dim] * dims[dim + 1], *dims[dim + 2 :])


def gathered_copies(value, axis, dim):
    blocks = copy_for_each(value, axis)
    return laid_out(blocks, dim)


def rows_for(lines, length):
    spare = -lines.shape[0] % length
    if not spare:
        return lines
    return jnp.concatenate([lines, jnp.zeros((spare, *lines.shape[1:]), lines.dtype)])


def total_of(value, axis):
    lines = value.reshape(-1, *value.shape[1:][-1:])
    padded = rows_for(lines, lax.axis_size(axis))
    own = lax.psum_scatter(padded, axis, scatter_dimension=0, tiled=True)
    whole = lax.all_gather(own, axis, axis=0, tiled=True)
    return whole[: len(lines)].reshape(value.shape)


def split_up(value, dim, length):
    dims = value.shape
    blocks = value.reshape(*dims[:dim], length, dims[dim] // length, *dims[dim + 1 :])
    return jnp.moveaxis(blocks, dim, 0)


def summed_on_arrival(value, axis, dim):
    blocks = split_up(value, dim, lax.axis_size(axis))
    arrived = lax.all_to_all(blocks, axis, split_axis=0, concat_axis=0, tiled=True)
    return arrived.sum(axis=0)


def local(hidden, latent, out_grad, up_weight, mb_tokens, slot_mb):
    slot_count = hidden.shape[1]
    capacity = hidden.shape[2]
    micro_count = mb_tokens.shape[1]
    row_total = slot_count * capacity
    slot_ids = slot_mb[0]
    lookup = slot_ids[:, None] == jnp.arange(micro_count, dtype=jnp.int32)[None, :]
    counts = jnp.sum(jnp.where(lookup, mb_tokens[0][None, :], 0), axis=1)
    valid_rows = jnp.arange(capacity, dtype=jnp.int32)[None, :] < counts[:, None]
    masked_grads = jnp.where(valid_rows[:, :, None], out_grad[0], jnp.zeros((), out_grad.dtype))
    masked_grads = masked_grads.reshape(row_total, -1)
    factors = gathered_copies(latent[0].reshape(row_total, -1), "tp", 1)
    partial_latent = lax.dot_general(
        masked_grads, up_weight, (((1,), (1,)), ((), ())), preferred_element_type=jnp.float32
    )
    latent_grad = total_of(partial_latent, "tp").astype(jnp.bfloat16)
    owner_part = lax.psum_scatter(
        lax.dot_general(
            factors, masked_grads, (((0,), (0,)), ((), ())), preferred_element_type=jnp.float32
        ),
        "mb",
        scatter_dimension=0,
        tiled=True,
    )
    up_grad = summed_on_arrival(owner_part, "dp", 0)
    hidden_rows = hidden[0].reshape(row_total, -1)
    down_term = lax.dot_general(
        hidden_rows, latent_grad, (((0,), (0,)), ((), ())), preferred_element_type=jnp.float32
    )
    down_share = summed_on_arrival(down_term, "dp", 1)
    own_index = lax.axis_index("mb")
    shard_rows = lax.all_gather(down_share[None], "mb", axis=0, tiled=True)
    positions = jnp.arange(shard_rows.shape[0], dtype=jnp.int32)
    weights_in = (positions <= own_index).astype(jnp.float32)
    running = jnp.einsum("k,kdr->dr", weights_in, shard_rows)
    return (up_grad, running[None])


def solution(mesh):
    return jax.shard_map(
        local,
        mesh=mesh,
        in_specs=(
            P("dp", "mb", None, "tp"),
            P("dp", "mb", None, "tp"),
            P("dp", "mb", None, "tp"),
            P(None, "tp"),
            P("dp", None),
            P("dp", "mb"),
        ),
        out_specs=(P(("mb", "dp"), "tp"), P("mb", "tp", "dp")),
        check_vma=False,
    )
```

profile of v0, /device:TPU:4, one launch (start us, length us, event | category | flops | bytes accessed | tf_op | source)
XLA Modules:
  0.0 198.9 jit_solution(7407583883337681670)
XLA Ops:
  8.1 1.0 fusion.5
  9.1 0.1 iota_compare_fusion
  9.2 2.5 %bitcast_select_fusion = bf16[1024,2048]{1,0:T(8,128)(2,1)S(1)} fusion(bf16[1,2,512,2048]{3,2,1,0:T(8,128)(2,1)} %param.8, pred[1024]{0:T(1024)(128)(4,1)S(1)} %lt.24), kind=kLoop, calls=%fused_computation | loop fusion | flops 2097152 | bytes 8389632 | tf_op jit(solution)/shard_map/jit(_where)/select_n | solution.py:59
  11.7 3.7 %fusion.8 = f32[1024,512]{1,0:T(8,128)} fusion(bf16[1024,2048]{1,0:T(8,128)(2,1)S(1)} %bitcast_select_fusion, bf16[512,2048]{1,0:T(8,128)(2,1)S(1)} %copy-done), kind=kOutput, calls=%fused_computation.13 | convolution fusion | flops 2147483648 | bytes 8388608 | tf_op jit(solution)/shard_map/dot_general | solution.py:62
  15.5 39.4 %reduce-scatter.5.cloned.1.call-done = f32[128,512]{1,0:T(8,128)} async-done(((f32[1024,512]{1,0:T(8,128)}), f32[128,512]{1,0:T(8,128)}) %reduce-scatter.5.cloned.1.call-update) | async-done | bytes 262160 | tf_op jit(solution)/shard_map/reduce_scatter | solution.py:33
  55.0 0.1 copy.12
  55.2 1.1 broadcast_in_dim.48
  56.3 3.6 %all-to-all-start = ((bf16[8,1024,64]{1,2,0:T(8,128)(2,1)}), bf16[8,1024,64]{1,2,0:T(8,128)(2,1)S(1)}, u32[]{:S(2)}, u32[]{:S(2)}) async-start(bf16[8,1024,64]{1,2,0:T(8,128)(2,1)} %broadcast_in_dim.48), calls=%async_computation | async-start | bytes 2097152 | tf_op jit(solution)/shard_map/all_to_all | solution.py:9
  59.9 4.5 %broadcast_select_fusion = bf16[1,2,512,2048]{3,2,1,0:T(8,128)(2,1)} fusion(bf16[1,2,512,2048]{3,2,1,0:T(8,128)(2,1)} %param.8, pred[2,512]{1,0:T(4,128)(4,1)S(1)} %iota_compare_fusion), kind=kLoop, calls=%fused_computation.1 | loop fusion | flops 2097152 | bytes 8389632 | tf_op jit(solution)/shard_map/jit(_where)/select_n | solution.py:59
  64.4 15.6 %all-to-all-done = bf16[8,1024,64]{1,2,0:T(8,128)(2,1)S(1)} async-done(((bf16[8,1024,64]{1,2,0:T(8,128)(2,1)}), bf16[8,1024,64]{1,2,0:T(8,128)(2,1)S(1)}, u32[]{:S(2)}, u32[]{:S(2)}) %all-to-all-start) | async-done | bytes 1048608 | tf_op jit(solution)/shard_map/all_to_all | solution.py:9
  80.0 6.6 %convolution_bitcast_fusion = f32[512,2048]{0,1:T(8,128)} fusion(bf16[1024,2048]{1,0:T(8,128)(2,1)} %bitcast.38, bf16[1024,512]{0,1:T(8,128)(2,1)S(1)} %bitcast.41), kind=kOutput, calls=%fused_computation.2 | convolution fusion | flops 2147483648 | bytes 9437184 | tf_op jit(solution)/shard_map/dot_general | solution.py:67
  86.6 5.4 %copy.15 = f32[512,2048]{1,0:T(8,128)} copy(f32[512,2048]{0,1:T(8,128)} %convolution_bitcast_fusion) | data formatting | bytes 8388608
  92.0 0.0 all-gather.6.cloned.1.call-start
  92.1 3.4 %fusion = f32[512,896]{1,0:T(8,128)S(1)} fusion(bf16[1024,896]{1,0:T(8,128)(2,1)} %bitcast.45, f32[1024,512]{1,0:T(8,128)} %all-gather.4.cloned.1.call-done), kind=kOutput, calls=%fused_computation.3 | convolution fusion | flops 940048384 | bytes 5767168 | tf_op jit(solution)/shard_map/dot_general | solution.py:76
  95.5 24.0 %all_to_all.15 = f32[4,896,128]{1,2,0:T(8,128)} all-to-all(f32[4,896,128]{1,2,0:T(8,128)S(1)} %bitcast.40), channel_id=1, replica_groups=mesh['mb'=8,'tp'=8,'dp'=4] {'dp'}, dimensions={0} | all-to-all | bytes 3670016 | tf_op jit(solution)/shard_map/all_to_all | solution.py:46
  119.5 2.4 %reduce_sum.29 = bf16[896,128]{0,1:T(8,128)(2,1)} reduce(f32[4,896,128]{1,2,0:T(8,128)} %all_to_all.15, f32[]{:T(128)} %constant.4.clone.1), dimensions={0}, to_apply=%region_4.5 | reduce | flops 344064 | bytes 2064388 | tf_op jit(solution)/shard_map/reduce_sum | solution.py:47
  122.0 24.7 %reduce-scatter.7.cloned.1.call-done = f32[64,2048]{1,0:T(8,128)} async-done(((f32[512,2048]{1,0:T(8,128)}), f32[64,2048]{1,0:T(8,128)}) %reduce-scatter.7.cloned.1.call-update) | async-done | bytes 524304 | tf_op jit(solution)/shard_map/reduce_scatter | solution.py:66
  146.7 4.8 %all-to-all-start.1 = ((f32[4,16,2048]{2,1,0:T(8,128)}), f32[4,16,2048]{2,1,0:T(8,128)S(1)}, u32[]{:S(2)}, u32[]{:S(2)}) async-start(f32[4,16,2048]{2,1,0:T(8,128)} %bitcast.43), calls=%async_computation.1 | async-start | bytes 1048576 | tf_op jit(solution)/shard_map/all_to_all | solution.py:46
  151.5 6.4 %all-to-all-done.1 = f32[4,16,2048]{2,1,0:T(8,128)S(1)} async-done(((f32[4,16,2048]{2,1,0:T(8,128)}), f32[4,16,2048]{2,1,0:T(8,128)S(1)}, u32[]{:S(2)}, u32[]{:S(2)}) %all-to-all-start.1) | async-done | bytes 524320 | tf_op jit(solution)/shard_map/all_to_all | solution.py:46
  157.8 0.7 reduce_sum.28
  158.5 29.4 %all-gather.6.cloned.1.call-done = bf16[7168,128]{0,1:T(8,128)(2,1)} async-done(((bf16[896,128]{0,1:T(8,128)(2,1)}), bf16[7168,128]{0,1:T(8,128)(2,1)}) %all-gather.6.cloned.1.call-update) | async-done | bytes 1835024 | tf_op jit(solution)/shard_map/all_gather | solution.py:81
  187.9 1.8 copy.18
  189.7 0.6 fusion.2
  190.4 1.1 copy.14
  (14 shorter events, 0.3 us)
Async XLA Ops:
  8.0 3.7 %copy-start = (bf16[512,2048]{1,0:T(8,128)(2,1)S(1)}, bf16[512,2048]{1,0:T(8,128)(2,1)}, u32[]{:S(2)}) copy-start(bf16[512,2048]{1,0:T(8,128)(2,1)} %param.9) | copy-start | bytes 6291460
  8.0 46.9 %reduce-scatter.5.cloned.1.call-start = ((), (), s32[]{:S(2)}) async-start(), calls=%async_computation.5 | async-start | bytes 2359296 | tf_op jit(solution)/shard_map/reduce_scatter | solution.py:33
  15.4 39.5 %copy-start.1 = (bf16[1,2,512,64]{2,3,1,0:T(8,128)(2,1)S(1)}, bf16[1,2,512,64]{2,3,1,0:T(8,128)(2,1)}, u32[]{:S(2)}) copy-start(bf16[1,2,512,64]{2,3,1,0:T(8,128)(2,1)} %param.7) | copy-start | bytes 393220
  15.5 76.6 %all-gather.4.cloned.1.call-start = ((), (), s32[]{:S(2)}) async-start(), calls=%async_computation.6 | async-start | bytes 2359296 | tf_op jit(solution)/shard_map/all_gather | solution.py:34
  56.3 23.7 %all-to-all-start = ((bf16[8,1024,64]{1,2,0:T(8,128)(2,1)}), bf16[8,1024,64]{1,2,0:T(8,128)(2,1)S(1)}, u32[]{:S(2)}, u32[]{:S(2)}) async-start(bf16[8,1024,64]{1,2,0:T(8,128)(2,1)} %broadcast_in_dim.48), calls=%async_computation | async-start | bytes 2097152 | tf_op jit(solution)/shard_map/all_to_all | solution.py:9
  59.8 86.8 %reduce-scatter.7.cloned.1.call-start = ((), (), s32[]{:S(2)}) async-start(), calls=%async_computation.8 | async-start | bytes 4718592 | tf_op jit(solution)/shard_map/reduce_scatter | solution.py:66
  92.0 95.9 %all-gather.6.cloned.1.call-start = ((), (), s32[]{:S(2)}) async-start(), calls=%async_computation.7 | async-start | bytes 2064384 | tf_op jit(solution)/shard_map/all_gather | solution.py:81
  146.7 11.2 %all-to-all-start.1 = ((f32[4,16,2048]{2,1,0:T(8,128)}), f32[4,16,2048]{2,1,0:T(8,128)S(1)}, u32[]{:S(2)}, u32[]{:S(2)}) async-start(f32[4,16,2048]{2,1,0:T(8,128)} %bitcast.43), calls=%async_computation.1 | async-start | bytes 1048576 | tf_op jit(solution)/shard_map/all_to_all | solution.py:46
Sparse Core Ops, SparseCore 0:
  15.6 39.3 reduce-scatter.4
  56.8 28.7 all-gather.3
Sparse Core Ops, SparseCore 1:
  92.1 54.5 reduce-scatter.6
  148.9 38.9 all-gather.5
where the time goes:
time: 199 us
  waiting for transfers between devices  116 us (58%)
  blocking collectives  24 us (12%)
  between operations  15.6 us (8%)
  matrix products  14.4 us (7%)
  other arithmetic  11.2 us (6%)
  local copies, waits for them, and re-layouts  9.6 us (5%)
  starting transfers between devices  8.52 us (4%)
    reduce_scatter x1, waiting for transfers between devices, total_of(): own = lax.psum_scatter(padded, axis, scatter_dimension=0, tiled=True)  39.4 us
    all_gather x1, waiting for transfers between devices, local(): shard_rows = lax.all_gather(down_share[None], 'mb', axis=0, tiled=True)  29.4 us
    reduce_scatter x1, waiting for transfers between devices, local(): lax.psum_scatter(lax.dot_general(factors, masked_grads, (((0,), (0,)), ((...  24.7 us
    all_to_all x1, blocking collectives, summed_on_arrival(): lax.all_to_all(blocks, axis, split_axis=0, concat_axis=0, tiled=True)  24 us
    all_to_all x1, waiting for transfers between devices, copy_for_each(): return lax.all_to_all(copies, axis, split_axis=0, concat_axis=0, tiled=True)  15.6 us
    unnamed x8, local copies, waits for them, and re-layouts  7.35 us
    select_n x2, other arithmetic, local(): jnp.where(valid_rows[:, :, None], out_grad[0], jnp.zeros((), out_grad.dty...  7.03 us
    dot_general x1, matrix products, local(): lax.dot_general(factors, masked_grads, (((0,), (0,)), ((), ())), preferre...  6.64 us
  transfers between devices with their start and end apart: 6, of which 5 were waited for; matrix products, arithmetic and copies ran while one was open for 12% of the time, Pallas kernels for 0%

commit v1 on v0

--- a/solution.py
+++ b/solution.py
@@ -78,7 +78,11 @@
     )
     down_share = summed_on_arrival(down_term, "dp", 1)
     own_index = lax.axis_index("mb")
-    shard_rows = lax.all_gather(down_share[None], "mb", axis=0, tiled=True)
+    row_data = down_share[None]
+    r1 = jnp.stack(jax.lax.axis_size("mb") * [row_data])
+    shard_rows = jnp.concatenate(
+        jax.lax.all_to_all(r1, concat_axis=0, split_axis=0, axis_name="mb"), 0
+    )
     positions = jnp.arange(shard_rows.shape[0], dtype=jnp.int32)
     weights_in = (positions <= own_index).astype(jnp.float32)
     running = jnp.einsum("k,kdr->dr", weights_in, shard_rows)

time: 199 us -> 223 us (1.12); the launches traced: 199 us -> 219 us
  waiting for transfers between devices: 116 us -> 131 us
  starting transfers between devices: 8.52 us -> 12.8 us
  matrix products: 14.4 us -> 17.3 us
    all_to_all x0 -> x1, waiting for transfers between devices: none -> 43.9 us  [local(): jax.lax.all_to_all(r1, concat_axis=0, split_axis=0, axis_name='mb')]
    all_gather x1 -> x0, waiting for transfers between devices: 29.4 us -> none  [local(): shard_rows = lax.all_gather(down_share[None], 'mb', axis=0, tiled=True)]
    all_to_all x0 -> x1, starting transfers between devices: none -> 4.36 us  [local(): jax.lax.all_to_all(r1, concat_axis=0, split_axis=0, axis_name='mb')]
    dot_general x1, matrix products: 0.62 us -> 3.51 us  [local(): running = jnp.einsum('k,kdr->dr', weights_in, shard_rows)]
    reduce_scatter x1, waiting for transfers between devices: 24.7 us -> 27.1 us  [local(): lax.psum_scatter(lax.dot_general(factors, masked_grads, (((0,), (0,)), ((...]
    unnamed x8 -> x7, local copies, waits for them, and re-layouts: 7.35 us -> 5.56 us
  transfers between devices with their start and end apart: 6 -> 6, of which waited for: 5 -> 5; matrix products, arithmetic and copies ran while one was open for 12% -> 11% of each run, Pallas kernels for 0% -> 0%
where the time goes in v1:
time: 223 us; the launch traced here: 219 us
  waiting for transfers between devices  131 us (59%)
  blocking collectives  24.1 us (11%)
  matrix products  17.3 us (8%)
  between operations  15.6 us (7%)
  starting transfers between devices  12.8 us (6%)
  other arithmetic  10.4 us (5%)
  local copies, waits for them, and re-layouts  8.32 us (4%)
    all_to_all x1, waiting for transfers between devices, local(): jax.lax.all_to_all(r1, concat_axis=0, split_axis=0, axis_name='mb')  43.9 us
    reduce_scatter x1, waiting for transfers between devices, total_of(): own = lax.psum_scatter(padded, axis, scatter_dimension=0, tiled=True)  39.4 us
    reduce_scatter x1, waiting for transfers between devices, local(): lax.psum_scatter(lax.dot_general(factors, masked_grads, (((0,), (0,)), ((...  27.1 us
    all_to_all x1, blocking collectives, summed_on_arrival(): lax.all_to_all(blocks, axis, split_axis=0, concat_axis=0, tiled=True)  24.1 us
    all_to_all x1, waiting for transfers between devices, copy_for_each(): return lax.all_to_all(copies, axis, split_axis=0, concat_axis=0, tiled=True)  15.6 us
    select_n x2, other arithmetic, local(): jnp.where(valid_rows[:, :, None], out_grad[0], jnp.zeros((), out_grad.dty...  7.02 us
    dot_general x1, matrix products, local(): lax.dot_general(factors, masked_grads, (((0,), (0,)), ((), ())), preferre...  6.63 us
    unnamed x7, local copies, waits for them, and re-layouts  5.56 us
  transfers between devices with their start and end apart: 6, of which 5 were waited for; matrix products, arithmetic and copies ran while one was open for 11% of the time, Pallas kernels for 0%

profile of v1, /device:TPU:4, one launch (start us, length us, event | category | flops | bytes accessed | tf_op | source)
XLA Modules:
  0.0 219.3 jit_solution(7451155161551556874)
XLA Ops:
  8.1 1.0 fusion.6
  9.1 0.1 iota_compare_fusion
  9.2 2.5 %bitcast_select_fusion = bf16[1024,2048]{1,0:T(8,128)(2,1)S(1)} fusion(bf16[1,2,512,2048]{3,2,1,0:T(8,128)(2,1)} %param.8, pred[1024]{0:T(1024)(128)(4,1)S(1)} %lt.24), kind=kLoop, calls=%fused_computation | loop fusion | flops 2097152 | bytes 8389632 | tf_op jit(solution)/shard_map/jit(_where)/select_n | solution.py:59
  11.7 3.7 %fusion.9 = f32[1024,512]{1,0:T(8,128)} fusion(bf16[1024,2048]{1,0:T(8,128)(2,1)S(1)} %bitcast_select_fusion, bf16[512,2048]{1,0:T(8,128)(2,1)S(1)} %copy-done), kind=kOutput, calls=%fused_computation.14 | convolution fusion | flops 2147483648 | bytes 8388608 | tf_op jit(solution)/shard_map/dot_general | solution.py:62
  15.5 39.4 %reduce-scatter.5.cloned.1.call-done = f32[128,512]{1,0:T(8,128)} async-done(((f32[1024,512]{1,0:T(8,128)}), f32[128,512]{1,0:T(8,128)}) %reduce-scatter.5.cloned.1.call-update) | async-done | bytes 262160 | tf_op jit(solution)/shard_map/reduce_scatter | solution.py:33
  55.0 0.1 copy.13
  55.2 1.1 broadcast_in_dim.45
  56.3 3.6 %all-to-all-start = ((bf16[8,1024,64]{1,2,0:T(8,128)(2,1)}), bf16[8,1024,64]{1,2,0:T(8,128)(2,1)S(1)}, u32[]{:S(2)}, u32[]{:S(2)}) async-start(bf16[8,1024,64]{1,2,0:T(8,128)(2,1)} %broadcast_in_dim.45), calls=%async_computation | async-start | bytes 2097152 | tf_op jit(solution)/shard_map/all_to_all | solution.py:9
  59.9 4.5 %broadcast_select_fusion = bf16[1,2,512,2048]{3,2,1,0:T(8,128)(2,1)} fusion(bf16[1,2,512,2048]{3,2,1,0:T(8,128)(2,1)} %param.8, pred[2,512]{1,0:T(4,128)(4,1)S(1)} %iota_compare_fusion), kind=kLoop, calls=%fused_computation.1 | loop fusion | flops 2097152 | bytes 8389632 | tf_op jit(solution)/shard_map/jit(_where)/select_n | solution.py:59
  64.4 15.6 %all-to-all-done = bf16[8,1024,64]{1,2,0:T(8,128)(2,1)S(1)} async-done(((bf16[8,1024,64]{1,2,0:T(8,128)(2,1)}), bf16[8,1024,64]{1,2,0:T(8,128)(2,1)S(1)}, u32[]{:S(2)}, u32[]{:S(2)}) %all-to-all-start) | async-done | bytes 1048608 | tf_op jit(solution)/shard_map/all_to_all | solution.py:9
  80.0 6.6 %convolution_bitcast_fusion = f32[512,2048]{0,1:T(8,128)} fusion(bf16[1024,2048]{1,0:T(8,128)(2,1)} %bitcast.35, bf16[1024,512]{0,1:T(8,128)(2,1)S(1)} %bitcast.37), kind=kOutput, calls=%fused_computation.4 | convolution fusion | flops 2147483648 | bytes 9437184 | tf_op jit(solution)/shard_map/dot_general | solution.py:67
  86.6 5.4 %copy.18 = f32[512,2048]{1,0:T(8,128)} copy(f32[512,2048]{0,1:T(8,128)} %convolution_bitcast_fusion) | data formatting | bytes 8388608
  92.1 3.4 %fusion.2 = f32[512,896]{1,0:T(8,128)S(1)} fusion(bf16[1024,896]{1,0:T(8,128)(2,1)} %bitcast.42, f32[1024,512]{1,0:T(8,128)} %all-gather.2.cloned.1.call-done), kind=kOutput, calls=%fused_computation.5 | convolution fusion | flops 940048384 | bytes 5767168 | tf_op jit(solution)/shard_map/dot_general | solution.py:76
  95.5 24.1 %all_to_all.20 = f32[4,896,128]{1,2,0:T(8,128)} all-to-all(f32[4,896,128]{1,2,0:T(8,128)S(1)} %bitcast.36), channel_id=1, replica_groups=mesh['mb'=8,'tp'=8,'dp'=4] {'dp'}, dimensions={0} | all-to-all | bytes 3670016 | tf_op jit(solution)/shard_map/all_to_all | solution.py:46
  119.5 27.1 %reduce-scatter.7.cloned.1.call-done = f32[64,2048]{1,0:T(8,128)} async-done(((f32[512,2048]{1,0:T(8,128)}), f32[64,2048]{1,0:T(8,128)}) %reduce-scatter.7.cloned.1.call-update) | async-done | bytes 524304 | tf_op jit(solution)/shard_map/reduce_scatter | solution.py:66
  146.7 4.8 %all-to-all-start.1 = ((f32[4,16,2048]{2,1,0:T(8,128)}), f32[4,16,2048]{2,1,0:T(8,128)S(1)}, u32[]{:S(2)}, u32[]{:S(2)}) async-start(f32[4,16,2048]{2,1,0:T(8,128)} %bitcast.39), calls=%async_computation.1 | async-start | bytes 1048576 | tf_op jit(solution)/shard_map/all_to_all | solution.py:46
  151.5 1.6 reduce_sum.29
  153.1 0.2 copy.15
  153.3 4.6 %all-to-all-done.1 = f32[4,16,2048]{2,1,0:T(8,128)S(1)} async-done(((f32[4,16,2048]{2,1,0:T(8,128)}), f32[4,16,2048]{2,1,0:T(8,128)S(1)}, u32[]{:S(2)}, u32[]{:S(2)}) %all-to-all-start.1) | async-done | bytes 524320 | tf_op jit(solution)/shard_map/all_to_all | solution.py:46
  157.9 1.5 stack.3
  159.4 4.4 %all-to-all-start.3 = ((bf16[8,1,896,128]{3,2,1,0:T(8,128)(2,1)}), bf16[8,1,896,128]{3,2,1,0:T(8,128)(2,1)}, u32[]{:S(2)}, u32[]{:S(2)}) async-start(bf16[8,1,896,128]{3,2,1,0:T(8,128)(2,1)} %stack.3), calls=%async_computation.4 | async-start | bytes 3670016 | tf_op jit(solution)/shard_map/all_to_all | solution.py:84
  163.7 0.7 reduce_sum.28
  164.4 43.9 %all-to-all-done.3 = bf16[8,1,896,128]{3,2,1,0:T(8,128)(2,1)} async-done(((bf16[8,1,896,128]{3,2,1,0:T(8,128)(2,1)}), bf16[8,1,896,128]{3,2,1,0:T(8,128)(2,1)}, u32[]{:S(2)}, u32[]{:S(2)}) %all-to-all-start.3) | async-done | bytes 1835040 | tf_op jit(solution)/shard_map/all_to_all | solution.py:84
  208.3 3.5 %fusion = f32[1,896,128]{2,0,1:T(1,128)} fusion(bf16[8,896,128]{2,1,0:T(8,128)(2,1)} %bitcast.13, s32[]{:T(128)S(6)} %axis_index.15), kind=kOutput, calls=%fused_computation.2 | convolution fusion | flops 1835016 | bytes 2293764 | tf_op jit(solution)/shard_map/k,kdr->dr/dot_general | solution.py:88
  (13 shorter events, 0.2 us)
Async XLA Ops:
  8.0 3.7 %copy-start = (bf16[512,2048]{1,0:T(8,128)(2,1)S(1)}, bf16[512,2048]{1,0:T(8,128)(2,1)}, u32[]{:S(2)}) copy-start(bf16[512,2048]{1,0:T(8,128)(2,1)} %param.9) | copy-start | bytes 6291460
  8.0 46.9 %reduce-scatter.5.cloned.1.call-start = ((), (), s32[]{:S(2)}) async-start(), calls=%async_computation.6 | async-start | bytes 2359296 | tf_op jit(solution)/shard_map/reduce_scatter | solution.py:33
  15.4 39.5 %copy-start.1 = (bf16[1,2,512,64]{2,3,1,0:T(8,128)(2,1)S(1)}, bf16[1,2,512,64]{2,3,1,0:T(8,128)(2,1)}, u32[]{:S(2)}) copy-start(bf16[1,2,512,64]{2,3,1,0:T(8,128)(2,1)} %param.7) | copy-start | bytes 393220
  15.5 76.6 %all-gather.2.cloned.1.call-start = ((), (), s32[]{:S(2)}) async-start(), calls=%async_computation.7 | async-start | bytes 2359296 | tf_op jit(solution)/shard_map/all_gather | solution.py:34
  56.3 23.7 %all-to-all-start = ((bf16[8,1024,64]{1,2,0:T(8,128)(2,1)}), bf16[8,1024,64]{1,2,0:T(8,128)(2,1)S(1)}, u32[]{:S(2)}, u32[]{:S(2)}) async-start(bf16[8,1024,64]{1,2,0:T(8,128)(2,1)} %broadcast_in_dim.45), calls=%async_computation | async-start | bytes 2097152 | tf_op jit(solution)/shard_map/all_to_all | solution.py:9
  59.8 86.9 %reduce-scatter.7.cloned.1.call-start = ((), (), s32[]{:S(2)}) async-start(), calls=%async_computation.8 | async-start | bytes 4718592 | tf_op jit(solution)/shard_map/reduce_scatter | solution.py:66
  146.7 11.2 %all-to-all-start.1 = ((f32[4,16,2048]{2,1,0:T(8,128)}), f32[4,16,2048]{2,1,0:T(8,128)S(1)}, u32[]{:S(2)}, u32[]{:S(2)}) async-start(f32[4,16,2048]{2,1,0:T(8,128)} %bitcast.39), calls=%async_computation.1 | async-start | bytes 1048576 | tf_op jit(solution)/shard_map/all_to_all | solution.py:46
  159.4 49.0 %all-to-all-start.3 = ((bf16[8,1,896,128]{3,2,1,0:T(8,128)(2,1)}), bf16[8,1,896,128]{3,2,1,0:T(8,128)(2,1)}, u32[]{:S(2)}, u32[]{:S(2)}) async-start(bf16[8,1,896,128]{3,2,1,0:T(8,128)(2,1)} %stack.3), calls=%async_computation.4 | async-start | bytes 3670016 | tf_op jit(solution)/shard_map/all_to_all | solution.py:84
Sparse Core Ops, SparseCore 0:
  15.6 39.3 reduce-scatter.4
  56.8 28.7 all-gather.1
Sparse Core Ops, SparseCore 1:
  92.1 54.5 reduce-scatter.6
